TPU v7x, 16 devices: a 4x2x1 block of a 4x4x8 slice. The times are simulated.
16 devices in a mesh: dp: 2 (over y, z), tp: 8 (over x, core).
Axes of the slice: x: 4, y: 2, z: 1, core: 2. Of those that a mesh axis runs over, the one named last changes fastest.
The devices are a block of a 4x4x8 slice.
Arguments:
- resid_in: bfloat16 [256, 5120], P('dp'), parts along dimension 0
- positions: int32 [256], P('dp'), parts along dimension 0
- k_cache: bfloat16 [256, 128, 8, 128], P('dp', None, 'tp'), parts along dimension 0
- v_cache: bfloat16 [256, 128, 8, 128], P('dp', None, 'tp'), parts along dimension 0
- gain_attn: bfloat16 [5120], replicated
- w_query: bfloat16 [5120, 4096], P(None, 'tp')
- w_key: bfloat16 [5120, 1024], P(None, 'tp')
- w_value: bfloat16 [5120, 1024], P(None, 'tp')
- w_out: bfloat16 [4096, 5120], P('tp')
- gain_mlp: bfloat16 [5120], replicated
- w_gate: bfloat16 [5120, 32768], P(None, 'tp')
- w_up: bfloat16 [5120, 32768], P(None, 'tp')
- w_down: bfloat16 [32768, 5120], P('tp')
Outputs:
- output 1: bfloat16 [256, 5120], P('dp'), parts along dimension 0
- output 2: bfloat16 [256, 128, 8, 128], P('dp', None, 'tp'), parts along dimension 0
- output 3: bfloat16 [256, 128, 8, 128], P('dp', None, 'tp'), parts along dimension 0
There are 2 independent parts. A program takes and returns all parts, laid end to end along the dimension named above; an argument that names none is the same for every part.
All inputs are finite; a program needn't handle non-finite values.
Results may differ from a plain program's by a relative error of at most 0.0105374.
Values sent between devices are 32-bit elements.
A program may use at most 768 MiB of HBM per device.

v0:
```python
import math
import jax
import jax.numpy as jnp
from jax import lax
from jax.sharding import PartitionSpec as P

EPS = 1e-5
ROPE_THETA = 500000.0
ROPE_FACTOR = 8.0
LOW_FACTOR = 1.0
HIGH_FACTOR = 4.0
ORIG_CTX = 8192.0


def rms_norm(rows_in, gain):
    rows_f = rows_in.astype(jnp.float32)
    mean_sq = jnp.mean(rows_f * rows_f, axis=-1, keepdims=True)
    return (rows_f * lax.rsqrt(mean_sq + EPS) * gain.astype(jnp.float32)).astype(jnp.bfloat16)


def rope_tables(positions, head_dim):
    half_dim = head_dim // 2
    exponents = jnp.arange(half_dim, dtype=jnp.float32) * (2.0 / head_dim)
    inv_freq = 1.0 / jnp.power(ROPE_THETA, exponents)
    wavelen = (2.0 * math.pi) / inv_freq
    smooth = (ORIG_CTX / wavelen - LOW_FACTOR) / (HIGH_FACTOR - LOW_FACTOR)
    blended = (1.0 - smooth) * inv_freq / ROPE_FACTOR + smooth * inv_freq
    inv_freq = jnp.where(wavelen < ORIG_CTX / HIGH_FACTOR, inv_freq,
                         jnp.where(wavelen > ORIG_CTX / LOW_FACTOR, inv_freq / ROPE_FACTOR, blended))
    angles = positions.astype(jnp.float32)[:, None] * inv_freq[None, :]
    return jnp.cos(angles), jnp.sin(angles)


def apply_rope(vectors, cos_t, sin_t):
    half_dim = vectors.shape[-1] // 2
    lower_half = vectors[..., :half_dim]
    upper_half = vectors[..., half_dim:]
    cos_b = cos_t[:, None, :]
    sin_b = sin_t[:, None, :]
    return jnp.concatenate([lower_half * cos_b - upper_half * sin_b,
                            upper_half * cos_b + lower_half * sin_b], axis=-1)


def attention_block(resid_in, positions, k_cache, v_cache, gain_attn, w_query, w_key, w_value):
    n_seqs = resid_in.shape[0]
    cache_len = k_cache.shape[1]
    kv_heads = k_cache.shape[2]
    head_dim = k_cache.shape[3]
    group_size = w_query.shape[1] // (kv_heads * head_dim)
    normed = rms_norm(resid_in, gain_attn)
    queries = jnp.dot(normed, w_query, preferred_element_type=jnp.float32).astype(jnp.bfloat16)
    key_new = jnp.dot(normed, w_key, preferred_element_type=jnp.float32).astype(jnp.bfloat16)
    value_new = jnp.dot(normed, w_value, preferred_element_type=jnp.float32).astype(jnp.bfloat16)
    cos_t, sin_t = rope_tables(positions, head_dim)
    queries = apply_rope(queries.reshape(n_seqs, kv_heads * group_size, head_dim).astype(jnp.float32), cos_t, sin_t)
    queries = queries.astype(jnp.bfloat16).reshape(n_seqs, kv_heads, group_size, head_dim)
    key_new = apply_rope(key_new.reshape(n_seqs, kv_heads, head_dim).astype(jnp.float32), cos_t, sin_t)
    key_new = key_new.astype(jnp.bfloat16)
    value_new = value_new.reshape(n_seqs, kv_heads, head_dim)
    slot_iota = lax.broadcasted_iota(jnp.int32, (n_seqs, cache_len), 1)
    slot_hit = (slot_iota == positions[:, None])[:, :, None, None]
    k_full = jnp.where(slot_hit, key_new[:, None], k_cache)
    v_full = jnp.where(slot_hit, value_new[:, None], v_cache)
    scores = jnp.einsum('bkgd,bskd->bkgs', queries, k_full, preferred_element_type=jnp.float32)
    scores = scores * (1.0 / math.sqrt(head_dim))
    valid = (slot_iota <= positions[:, None])[:, None, None, :]
    scores = jnp.where(valid, scores, -jnp.inf)
    attn_prob = jax.nn.softmax(scores, axis=-1).astype(jnp.bfloat16)
    attn_out = jnp.einsum('bkgs,bskd->bkgd', attn_prob, v_full, preferred_element_type=jnp.float32)
    attn_out = attn_out.astype(jnp.bfloat16).reshape(n_seqs, kv_heads * group_size * head_dim)
    return attn_out, k_full, v_full


def gated_hidden(normed, w_gate, w_up):
    gate_proj = jnp.dot(normed, w_gate, preferred_element_type=jnp.float32).astype(jnp.bfloat16)
    up_proj = jnp.dot(normed, w_up, preferred_element_type=jnp.float32).astype(jnp.bfloat16)
    return (jax.nn.silu(gate_proj.astype(jnp.float32)) * up_proj.astype(jnp.float32)).astype(jnp.bfloat16)


def solution(mesh):
    def layer_local(resid_in, positions, k_cache, v_cache, gain_attn, w_query, w_key, w_value,
                    w_out, gain_mlp, w_gate, w_up, w_down):
        attn_out, k_full, v_full = attention_block(resid_in, positions, k_cache, v_cache,
                                                   gain_attn, w_query, w_key, w_value)
        y_part = jnp.dot(attn_out, w_out, preferred_element_type=jnp.float32)
        y_sum = lax.psum(y_part, 'tp')
        resid_mid = (resid_in.astype(jnp.float32) + y_sum).astype(jnp.bfloat16)
        hidden = gated_hidden(rms_norm(resid_mid, gain_mlp), w_gate, w_up)
        z_part = jnp.dot(hidden, w_down, preferred_element_type=jnp.float32)
        z_sum = lax.psum(z_part, 'tp')
        resid_out = (resid_mid.astype(jnp.float32) + z_sum).astype(jnp.bfloat16)
        return resid_out, k_full, v_full

    row_spec = P('dp', None)
    cache_spec = P('dp', None, 'tp', None)
    col_spec = P(None, 'tp')
    split_rows = P('tp', None)
    return jax.shard_map(layer_local, mesh=mesh,
                         in_specs=(row_spec, P('dp'), cache_spec, cache_spec, P(), col_spec, col_spec,
                                   col_spec, split_rows, P(), col_spec, col_spec, split_rows),
                         out_specs=(row_spec, cache_spec, cache_spec), check_vma=False)
```

profile of v0, /device:TPU:113, one launch (start us, length us, event | category | flops | bytes accessed | tf_op | source)
XLA Modules:
  0.0 219.7 jit_solution(11798122712279228227)
XLA Ops:
  7.2 0.0 copy-start
  7.2 0.0 copy-start.3
  7.2 0.1 all-reduce.3.cloned.1.call-start
  7.3 0.0 copy-start.6
  7.3 0.8 convert_element_type.89
  8.1 1.0 iota_compare_fusion.1
  9.1 1.7 fusion.9
  10.8 0.7 convert_element_type.84
  11.5 0.0 copy-done
  11.5 1.9 convolution_convert_fusion.3
  13.4 0.0 copy-done.3
  13.4 0.0 copy-done.6
  13.4 0.8 fusion.30
  14.2 0.3 multiply_cosine_fusion
  14.5 0.2 fusion.51
  14.7 0.1 copy.16
  14.8 3.4 %fusion.28 = f32[128,512]{1,0:T(8,128)S(1)} fusion(bf16[5120,512]{1,0:T(8,128)(2,1)} %param.18, bf16[128,5120]{1,0:T(8,128)(2,1)S(1)} %copy-done.3, f32[5120]{0:T(1024)S(1)} %convert_element_type.84, f32[128]{0:T(128)S(1)} %add_rsqrt_fusion.1), kind=kOutput, calls=%fused_computation.33 | convolution fusion | flops 673841152 | bytes 6836736 | tf_op jit(solution)/shard_map/dot_general | solution.py:51
  18.2 0.1 reshape.252
  18.3 0.3 subtract_convert_fusion
  18.6 8.5 %broadcast_select_fusion.1 = (bf16[128,128,1,128]{3,1,2,0:T(8,128)(2,1)S(1)}, bf16[128,128,1,128]{3,1,2,0:T(8,128)(2,1)}) fusion(bf16[128,128,1,128]{3,1,2,0:T(8,128)(2,1)} %param.15, pred[128,128]{1,0:T(8,128)(4,1)S(1)} %get-tuple-element.14, bf16[128,128]{1,0:T(8,128)(2,1)S(1)} %copy.16, bf16[128,128,1,128]{3,1,2,0:T(8,128)(2,1)} %param.16, ...), kind=kLoop, calls=%fused_computation.12 | loop fusion | flops 4194304 | bytes 16859136 | tf_op jit(solution)/shard_map/jit(_where)/select_n | solution.py:62
  27.1 0.0 copy-start.2
  27.1 2.0 copy-done.2
  29.1 2.3 %fusion.22 = f32[128,4,128]{2,1,0:T(4,128)S(1)} fusion(bf16[128,128,1,128]{3,1,2,0:T(8,128)(2,1)S(1)} %get-tuple-element.9, bf16[128,4,64]{2,1,0:T(4,128)(2,1)S(1)} %get-tuple-element.6, bf16[128,4,64]{2,1,0:T(4,128)(2,1)S(1)} %get-tuple-element.5, pred[128,128]{1,0:T(8,128)(4,1)S(1)} %get-tuple-element.13), kind=kOutput, calls=%fused_computation.30 | convolution fusion | flops 17170432 | bytes 4603904 | tf_op jit(solution)/shard_map/bkgd,bskd->bkgs/dot_general | solution.py:64
  31.4 0.4 fusion.58
  31.8 4.0 %fusion.25 = bf16[128,4,128]{2,1,0:T(4,128)(2,1)S(1)} fusion(bf16[128,128,1,128]{3,1,2,0:T(8,128)(2,1)} %get-tuple-element.10, f32[128,4]{1,0:T(8,128)S(1)} %fusion.58, f32[128,4,128]{2,1,0:T(4,128)S(1)} %fusion.22), kind=kOutput, calls=%fused_computation.31 | convolution fusion | flops 17040000 | bytes 4589568 | tf_op jit(solution)/shard_map/bkgs,bskd->bkgd/dot_general | solution.py:69
  35.8 4.9 %fusion.35 = f32[128,5120]{1,0:T(8,128)} fusion(bf16[512,5120]{1,0:T(8,128)(2,1)} %param.21, bf16[16,8,4,128]{3,2,1,0:T(4,128)(2,1)S(1)} %bitcast.34), kind=kOutput, calls=%fused_computation.42 | convolution fusion | flops 671088640 | bytes 7995392 | tf_op jit(solution)/shard_map/dot_general | solution.py:85
  40.7 0.0 copy-start.5
  40.7 0.0 copy-start.4
  40.7 0.1 all-reduce.3.cloned.1.call-update
  40.7 0.2 all-reduce.5.cloned.1.call-start
  41.0 0.4 copy-done.5
  41.4 59.6 %all-reduce.3.cloned.1.call-done = f32[128,5120]{1,0:T(8,128)} async-done(((f32[128,5120]{1,0:T(8,128)}), f32[128,5120]{1,0:T(8,128)}) %all-reduce.3.cloned.1.call-update) | async-done | bytes 2621456 | tf_op jit(solution)/shard_map/psum | solution.py:86
  101.0 0.0 copy-done.4
  101.0 2.2 %fusion.13 = (f32[128]{0:T(128)S(1)}, bf16[128,5120]{1,0:T(8,128)(2,1)S(1)}) fusion(f32[128,5120]{1,0:T(8,128)} %all-reduce.3.cloned.1.call-done, bf16[128,5120]{1,0:T(8,128)(2,1)S(1)} %copy-done.4), kind=kLoop, calls=%fused_computation.23 | loop fusion | flops 3932032 | bytes 5243392 | tf_op jit(solution)/shard_map/reduce_sum | solution.py:17
  103.2 17.3 %fusion.4 = f32[128,4096]{1,0:T(8,128)} fusion(bf16[5120,4096]{1,0:T(8,128)(2,1)} %param.23, bf16[128,5120]{1,0:T(8,128)(2,1)S(1)} %get-tuple-element.4, f32[5120]{0:T(1024)S(1)} %convert_element_type.98, f32[128]{0:T(128)S(1)} %add_rsqrt_fusion), kind=kOutput, calls=%fused_computation.6 | convolution fusion | flops 5372379136 | bytes 45371904 | tf_op jit(solution)/shard_map/dot_general | solution.py:75
  120.5 30.3 %fusion.31 = f32[128,5120]{1,0:T(8,128)} fusion(bf16[4096,5120]{1,0:T(8,128)(2,1)} %param.25, bf16[5120,4096]{1,0:T(8,128)(2,1)} %param.24, f32[128,4096]{1,0:T(8,128)} %fusion.4, bf16[128,5120]{1,0:T(8,128)(2,1)S(1)} %get-tuple-element.4, f32[5120]{0:T(1024)S(1)} %convert_element_type.98, f32[128]{0:T(128)S(1)} %add_rsqrt_fusion), kind=kOutput, calls=%fused_computation.38 | convolution fusion | flops 10744233984 | bytes 89936384 | tf_op jit(solution)/shard_map/dot_general | solution.py:89
  150.8 0.1 all-reduce.5.cloned.1.call-update
  150.9 0.0 copy-start.1
  150.9 58.9 %all-reduce.5.cloned.1.call-done = f32[128,5120]{1,0:T(8,128)} async-done(((f32[128,5120]{1,0:T(8,128)}), f32[128,5120]{1,0:T(8,128)}) %all-reduce.5.cloned.1.call-update) | async-done | bytes 2621456 | tf_op jit(solution)/shard_map/psum | solution.py:90
  209.8 3.1 %fusion.16 = bf16[128,5120]{1,0:T(8,128)(2,1)} fusion(f32[128,5120]{1,0:T(8,128)} %all-reduce.5.cloned.1.call-done, bf16[128,5120]{1,0:T(8,128)(2,1)S(1)} %get-tuple-element.4), kind=kLoop, calls=%fused_computation.26 | loop fusion | flops 1966080 | bytes 5242880 | tf_op jit(solution)/shard_map/convert_element_type | solution.py:91
  212.9 0.0 copy-done.1
  (5 shorter events, 0.0 us)
Async XLA Ops:
  7.2 4.3 %copy-start = (bf16[5120,128]{1,0:T(8,128)(2,1)S(1)}, bf16[5120,128]{1,0:T(8,128)(2,1)}, u32[]{:S(2)}) copy-start(bf16[5120,128]{1,0:T(8,128)(2,1)} %param.20) | copy-start | bytes 3932164
  7.2 6.2 %copy-start.3 = (bf16[128,5120]{1,0:T(8,128)(2,1)S(1)}, bf16[128,5120]{1,0:T(8,128)(2,1)}, u32[]{:S(2)}) copy-start(bf16[128,5120]{1,0:T(8,128)(2,1)} %param.13) | copy-start | bytes 3932164
  7.2 93.8 %all-reduce.3.cloned.1.call-start = ((), (), s32[]{:S(2)}) async-start(), calls=%async_computation | async-start | bytes 5242880 | tf_op jit(solution)/shard_map/psum | solution.py:86
  7.3 6.1 %copy-start.6 = (bf16[5120,128]{1,0:T(8,128)(2,1)S(1)}, bf16[5120,128]{1,0:T(8,128)(2,1)}, u32[]{:S(2)}) copy-start(bf16[5120,128]{1,0:T(8,128)(2,1)} %param.19) | copy-start | bytes 3932164
  27.1 2.0 copy-start.2
  40.7 0.7 copy-start.5
  40.7 60.3 %copy-start.4 = (bf16[128,5120]{1,0:T(8,128)(2,1)S(1)}, bf16[128,5120]{1,0:T(8,128)(2,1)}, u32[]{:S(2)}) copy-start(bf16[128,5120]{1,0:T(8,128)(2,1)} %param.13) | copy-start | bytes 3932164
  40.7 169.1 %all-reduce.5.cloned.1.call-start = ((), (), s32[]{:S(2)}) async-start(), calls=%async_computation.1 | async-start | bytes 5242880 | tf_op jit(solution)/shard_map/psum | solution.py:90
  150.9 62.0 %copy-start.1 = (bf16[5120,128]{1,0:T(8,128)(2,1)S(1)}, bf16[5120,128]{1,0:T(8,128)(2,1)}, u32[]{:S(2)}) copy-start(bf16[5120,128]{1,0:T(8,128)(2,1)} %param.20) | copy-start | bytes 3932164
Sparse Core Ops, SparseCore 0:
  40.9 60.0 all-reduce.2
  151.0 58.7 all-reduce.4
where the time goes:
time: 222 us; the launch traced here: 220 us
  waiting for transfers between devices  119 us (54%)
  matrix products  64.8 us (29%)
  other arithmetic  19.1 us (9%)
  between operations  14.2 us (6%)
  local copies, waits for them, and re-layouts  2.63 us (1%)
    psum x1, waiting for transfers between devices, layer_local(): y_sum = lax.psum(y_part, 'tp')  59.6 us
    psum x1, waiting for transfers between devices, layer_local(): z_sum = lax.psum(z_part, 'tp')  58.9 us
    dot_general x1, matrix products, layer_local(): z_part = jnp.dot(hidden, w_down, preferred_element_type=jnp.float32)  30.3 us
    dot_general x1, matrix products, gated_hidden(): jnp.dot(normed, w_gate, preferred_element_type=jnp.float32)  17.3 us
    select_n x1, other arithmetic, attention_block(): k_full = jnp.where(slot_hit, key_new[:, None], k_cache)  8.49 us
    dot_general x1, matrix products, layer_local(): y_part = jnp.dot(attn_out, w_out, preferred_element_type=jnp.float32)  4.88 us
  transfers between devices with their start and end apart: 2, of which 2 were waited for; matrix products, arithmetic and copies ran while one was open for 0% of the time, Pallas kernels for 0%

commit v1 on v0

--- a/solution.py
+++ b/solution.py
@@ -1,7 +1,10 @@
+import functools
 import math
 import jax
 import jax.numpy as jnp
 from jax import lax
+from jax.experimental import pallas as pl
+from jax.experimental.pallas import tpu as pltpu
 from jax.sharding import PartitionSpec as P
 
 EPS = 1e-5
@@ -10,6 +13,13 @@
 LOW_FACTOR = 1.0
 HIGH_FACTOR = 4.0
 ORIG_CTX = 8192.0
+
+MESH = pl.DeviceIdType.MESH
+BLK = 512
+SLOTS = 11
+LAG_D, LAG_1, LAG_2 = 3, 7, 11
+GLAG_2, GLAG_3 = 3, 5
+ZLAGS = (1, 3, 5, 7, 9, 11)
 
 
 def rms_norm(rows_in, gain):
@@ -71,10 +81,262 @@
     return attn_out, k_full, v_full
 
 
-def gated_hidden(normed, w_gate, w_up):
-    gate_proj = jnp.dot(normed, w_gate, preferred_element_type=jnp.float32).astype(jnp.bfloat16)
-    up_proj = jnp.dot(normed, w_up, preferred_element_type=jnp.float32).astype(jnp.bfloat16)
-    return (jax.nn.silu(gate_proj.astype(jnp.float32)) * up_proj.astype(jnp.float32)).astype(jnp.bfloat16)
+def mlp_kernel(dims, o_ref, resid_ref, gain_ref, wo_ref, wg_ref, wu_ref, wd_ref, out_ref,
+               ring, ybuf, r_d, r_1, r_2, hbuf, acc_g, acc_u, hidden, x_own, rows_own,
+               w_sem, l_sem, snd, rcv):
+    n_ch, n_fb, rows = dims
+    me = lax.axis_index('tp')
+    core = lax.rem(me, 2)
+    chip = me // 2
+    apair = chip // 2
+    bpair = lax.rem((chip + 1) // 2, 2)
+    chip_a = chip + 1 - 2 * lax.rem(chip, 2)
+    chip_b = 3 - chip
+    hi = bpair + core * (apair - bpair)
+    lo = apair + core * (bpair - apair)
+    first = 2 * (chip_a + core * (chip_b - chip_a)) + core
+    second = 2 * (chip_b + core * (chip_a - chip_b)) + core
+    mate = 2 * chip + 1 - core
+    half = 4 * core
+    own = half + 2 * hi + lo
+
+    def remote(stage, u, src, dst, dev):
+        return pltpu.make_async_remote_copy(src_ref=src, dst_ref=dst, send_sem=snd.at[stage, u], recv_sem=rcv.at[stage, u],
+                                            device_id={'tp': dev}, device_id_type=MESH)
+
+    def s_d(u):
+        return remote(0, u, ybuf.at[u, pl.ds(4 - half, 4)], r_d.at[u], mate)
+
+    def s_1(u):
+        return remote(1, u, ybuf.at[u, pl.ds(half + 2 - 2 * hi, 2)], r_1.at[u], first)
+
+    def s_2(u):
+        return remote(2, u, ybuf.at[u, half + 2 * hi + 1 - lo], r_2.at[u], second)
+
+    def g_1(u):
+        return remote(3, u, hbuf.at[u, own], hbuf.at[u, own], second)
+
+    def g_2(u):
+        return remote(4, u, hbuf.at[u, pl.ds(half + 2 * hi, 2)], hbuf.at[u, pl.ds(half + 2 * hi, 2)], first)
+
+    def g_3(u):
+        return remote(5, u, hbuf.at[u, pl.ds(half, 4)], hbuf.at[u, pl.ds(half, 4)], mate)
+
+    def load_out(b, slot, idx):
+        return pltpu.make_async_copy(wo_ref.at[:, pl.ds(pl.multiple_of(b * BLK, BLK), BLK)], ring.at[slot, idx], w_sem.at[slot])
+
+    def issue(load):
+        slot = lax.rem(load, SLOTS)
+        seq = load - 2
+
+        def rows_of(w_ref, k):
+            for b in range(n_fb):
+                pltpu.make_async_copy(w_ref.at[pl.ds(pl.multiple_of(k * BLK, BLK), BLK), pl.ds(b * BLK, BLK)],
+                                      ring.at[slot, b], w_sem.at[slot]).start()
+
+        @pl.when((seq < 2 * n_ch) & (lax.rem(seq, 2) == 0))
+        def _():
+            rows_of(wg_ref, seq // 2)
+
+        @pl.when((seq < 2 * n_ch) & (lax.rem(seq, 2) == 1))
+        def _():
+            rows_of(wu_ref, seq // 2)
+
+        @pl.when((seq >= 2 * n_ch) & (seq < 3 * n_ch))
+        def _():
+            for b in range(n_fb):
+                pltpu.make_async_copy(wd_ref.at[pl.ds(b * BLK, BLK), pl.ds(pl.multiple_of((seq - 2 * n_ch) * BLK, BLK), BLK)],
+                                      ring.at[slot, b], w_sem.at[slot]).start()
+
+    def wait_load(load):
+        slot = lax.rem(load, SLOTS)
+        pltpu.make_async_copy(ring.at[slot], ring.at[slot], w_sem.at[slot]).wait()
+        return slot
+
+    for b in range(n_fb):
+        load_out(b, 0, b).start()
+    for b in range(n_fb, n_ch):
+        load_out(b, 1, b - n_fb).start()
+    row_copy = pltpu.make_async_copy(resid_ref.at[pl.ds(pl.multiple_of(own * rows, rows), rows)], rows_own, l_sem)
+    row_copy.start()
+
+    def first_loads(i, c):
+        issue(i)
+        return c
+    lax.fori_loop(2, SLOTS, first_loads, 0)
+
+    barrier = pltpu.get_barrier_semaphore()
+    for dev in (mate, first, second):
+        pl.semaphore_signal(barrier, inc=1, device_id={'tp': dev}, device_id_type=MESH)
+    pl.semaphore_wait(barrier, 3)
+
+    def at(t, lag, fn):
+        @pl.when((t >= lag) & (t < lag + n_ch))
+        def _():
+            fn(t - lag)
+
+    def after_d(u):
+        s_d(u).wait_recv()
+        ybuf[u, pl.ds(half, 4)] += r_d[u]
+        s_1(u).start()
+
+    def after_1(u):
+        s_1(u).wait_recv()
+        ybuf[u, pl.ds(half + 2 * hi, 2)] += r_1[u]
+        s_2(u).start()
+
+    wait_load(0)
+    pltpu.make_async_copy(ring.at[1, pl.ds(0, n_ch - n_fb)], ring.at[1, pl.ds(0, n_ch - n_fb)], w_sem.at[1]).wait()
+
+    def step_y(t, c):
+        def make(u):
+            blk = ring[u // n_fb, lax.rem(u, n_fb)]
+            y = jnp.dot(o_ref[...], blk, preferred_element_type=jnp.float32)
+            ybuf[u] = y.reshape(8, rows, BLK)
+            s_d(u).start()
+        at(t, 0, make)
+
+        @pl.when(t == n_ch)
+        def _():
+            issue(SLOTS)
+            issue(SLOTS + 1)
+        at(t, LAG_D, after_d)
+        at(t, LAG_1, after_1)
+
+        def done(u):
+            s_2(u).wait_recv()
+            x_own[u] = ybuf[u, own] + r_2[u]
+        at(t, LAG_2, done)
+        return c
+    lax.fori_loop(0, n_ch + LAG_2, step_y, 0)
+
+    def drain(u, c):
+        s_d(u).wait_send()
+        s_1(u).wait_send()
+        s_2(u).wait_send()
+        return c
+    lax.fori_loop(0, n_ch, drain, 0)
+
+    row_copy.wait()
+    total = jnp.zeros((rows, 1), jnp.float32)
+    for u in range(n_ch):
+        x1 = (rows_own[:, u * BLK:(u + 1) * BLK].astype(jnp.float32) + x_own[u]).astype(jnp.bfloat16).astype(jnp.float32)
+        x_own[u] = x1
+        total += jnp.sum(x1 * x1, axis=-1, keepdims=True)
+    inv = lax.rsqrt(total * (1.0 / (n_ch * BLK)) + EPS)
+    for u in range(n_ch):
+        gain = gain_ref[:, u * BLK:(u + 1) * BLK].astype(jnp.float32)
+        hbuf[u, own] = (x_own[u] * inv * gain).astype(jnp.bfloat16).astype(jnp.float32)
+        g_1(u).start()
+
+    acc_g[...] = jnp.zeros_like(acc_g)
+    acc_u[...] = jnp.zeros_like(acc_u)
+
+    def step_g(t, c):
+        def fwd_1(u):
+            g_1(u).wait_recv()
+            g_2(u).start()
+        at(t, 0, fwd_1)
+
+        def fwd_2(u):
+            g_2(u).wait_recv()
+            g_3(u).start()
+        at(t, GLAG_2, fwd_2)
+
+        def compute(u):
+            g_3(u).wait_recv()
+            h_k = hbuf[u].reshape(8 * rows, BLK).astype(jnp.bfloat16)
+            for which, acc in ((0, acc_g), (1, acc_u)):
+                load = 2 + 2 * u + which
+                slot = wait_load(load)
+                for b in range(n_fb):
+                    acc[b] += jnp.dot(h_k, ring[slot, b], preferred_element_type=jnp.float32)
+                issue(load + SLOTS)
+        at(t, GLAG_3, compute)
+        return c
+    lax.fori_loop(0, n_ch + GLAG_3, step_g, 0)
+
+    def drain_g(u, c):
+        g_1(u).wait_send()
+        g_2(u).wait_send()
+        g_3(u).wait_send()
+        return c
+    lax.fori_loop(0, n_ch, drain_g, 0)
+
+    for b in range(n_fb):
+        gate = acc_g[b].astype(jnp.bfloat16).astype(jnp.float32)
+        up = acc_u[b].astype(jnp.bfloat16).astype(jnp.float32)
+        hidden[:, b * BLK:(b + 1) * BLK] = (gate * jax.nn.sigmoid(gate) * up).astype(jnp.bfloat16)
+
+    def step_z(t, c):
+        def make(u):
+            slot = wait_load(2 + 2 * n_ch + u)
+            z = jnp.dot(hidden[...], ring[slot].reshape(n_fb * BLK, BLK), preferred_element_type=jnp.float32)
+            ybuf[u] = z.reshape(8, rows, BLK)
+            s_d(u).start()
+        at(t, 0, make)
+        at(t, ZLAGS[0], after_d)
+        at(t, ZLAGS[1], after_1)
+
+        def done(u):
+            s_2(u).wait_recv()
+            hbuf[u, own] = (x_own[u] + (ybuf[u, own] + r_2[u])).astype(jnp.bfloat16).astype(jnp.float32)
+            g_1(u).start()
+        at(t, ZLAGS[2], done)
+
+        def fwd_1(u):
+            g_1(u).wait_recv()
+            g_2(u).start()
+        at(t, ZLAGS[3], fwd_1)
+
+        def fwd_2(u):
+            g_2(u).wait_recv()
+            g_3(u).start()
+        at(t, ZLAGS[4], fwd_2)
+
+        def write(u):
+            g_3(u).wait_recv()
+            out_ref[:, pl.ds(pl.multiple_of(u * BLK, BLK), BLK)] = hbuf[u].reshape(8 * rows, BLK).astype(jnp.bfloat16)
+        at(t, ZLAGS[5], write)
+        return c
+    lax.fori_loop(0, n_ch + ZLAGS[5], step_z, 0)
+    lax.fori_loop(0, n_ch, drain, 0)
+    lax.fori_loop(0, n_ch, drain_g, 0)
+
+
+def mlp_part(attn_out, resid_in, gain_mlp, w_out, w_gate, w_up, w_down):
+    n_seqs, model = resid_in.shape
+    ffn = w_gate.shape[1]
+    n_ch, n_fb, rows = model // BLK, ffn // BLK, n_seqs // 8
+    f32, bf16 = jnp.float32, jnp.bfloat16
+    any_spec = pl.BlockSpec(memory_space=pltpu.HBM)
+    vmem_spec = pl.BlockSpec(memory_space=pltpu.VMEM)
+    return pl.pallas_call(
+        functools.partial(mlp_kernel, (n_ch, n_fb, rows)),
+        out_shape=jax.ShapeDtypeStruct((n_seqs, model), bf16),
+        in_specs=[vmem_spec, any_spec, vmem_spec, any_spec, any_spec, any_spec, any_spec],
+        out_specs=vmem_spec,
+        scratch_shapes=[
+            pltpu.VMEM((SLOTS, n_fb, BLK, BLK), bf16),
+            pltpu.VMEM((n_ch, 8, rows, BLK), f32),
+            pltpu.VMEM((n_ch, 4, rows, BLK), f32),
+            pltpu.VMEM((n_ch, 2, rows, BLK), f32),
+            pltpu.VMEM((n_ch, rows, BLK), f32),
+            pltpu.VMEM((n_ch, 8, rows, BLK), f32),
+            pltpu.VMEM((n_fb, n_seqs, BLK), f32),
+            pltpu.VMEM((n_fb, n_seqs, BLK), f32),
+            pltpu.VMEM((n_seqs, ffn), bf16),
+            pltpu.VMEM((n_ch, rows, BLK), f32),
+            pltpu.VMEM((rows, model), bf16),
+            pltpu.SemaphoreType.DMA((SLOTS,)),
+            pltpu.SemaphoreType.DMA,
+            pltpu.SemaphoreType.DMA((6, n_ch)),
+            pltpu.SemaphoreType.DMA((6, n_ch)),
+        ],
+        compiler_params=pltpu.CompilerParams(collective_id=0, has_side_effects=True, vmem_limit_bytes=66_900_000),
+        cost_estimate=pl.CostEstimate(flops=6 * n_seqs * model * ffn, bytes_accessed=6 * model * ffn, transcendentals=0),
+        name='out_mlp',
+    )(attn_out, resid_in, gain_mlp.reshape(1, model), w_out, w_gate, w_up, w_down)
 
 
 def solution(mesh):
@@ -82,13 +344,7 @@
                     w_out, gain_mlp, w_gate, w_up, w_down):
         attn_out, k_full, v_full = attention_block(resid_in, positions, k_cache, v_cache,
                                                    gain_attn, w_query, w_key, w_value)
-        y_part = jnp.dot(attn_out, w_out, preferred_element_type=jnp.float32)
-        y_sum = lax.psum(y_part, 'tp')
-        resid_mid = (resid_in.astype(jnp.float32) + y_sum).astype(jnp.bfloat16)
-        hidden = gated_hidden(rms_norm(resid_mid, gain_mlp), w_gate, w_up)
-        z_part = jnp.dot(hidden, w_down, preferred_element_type=jnp.float32)
-        z_sum = lax.psum(z_part, 'tp')
-        resid_out = (resid_mid.astype(jnp.float32) + z_sum).astype(jnp.bfloat16)
+        resid_out = mlp_part(attn_out, resid_in, gain_mlp, w_out, w_gate, w_up, w_down)
         return resid_out, k_full, v_full
 
     row_spec = P('dp', None)

time: 222 us -> 115 us (0.52)
  waiting for transfers between devices: 119 us -> 0 us
  Pallas kernels: 0 us -> 81.2 us
  matrix products: 64.8 us -> 12.7 us
  between operations: 14.2 us -> 0.77 us
  other arithmetic: 19.1 us -> 13 us
  local copies, waits for them, and re-layouts: 2.63 us -> 6.68 us
    psum x2 -> x0, waiting for transfers between devices: 118 us -> none  [the longest x1 59.6 us: layer_local(): y_sum = lax.psum(y_part, 'tp')]
    pallas_call x0 -> x1, Pallas kernels: none -> 81.2 us  [mlp_part(): pl.pallas_call(functools.partial(mlp_kernel, (n_ch, n_fb, rows)), out_sha...]
    dot_general x3 -> x0, matrix products: 52.5 us -> none  [the longest x1 30.3 us: layer_local(): z_part = jnp.dot(hidden, w_down, preferred_element_type=jnp.float32)]
    convert_element_type x1 -> x0, other arithmetic: 3.05 us -> none  [layer_local(): resid_out = (resid_mid.astype(jnp.float32) + z_sum).astype(jnp.bfloat16)]
    unnamed x14 -> x10, local copies, waits for them, and re-layouts: 2.43 us -> 5.17 us
  transfers between devices with their start and end apart: 2 -> 0, of which waited for: 2 -> 0; matrix products, arithmetic and copies ran while one was open for 0% -> 0% of each run, Pallas kernels for 0% -> 0%
where the time goes in v1:
time: 115 us; the launch traced here: 114 us
  Pallas kernels  81.2 us (71%)
  other arithmetic  13 us (11%)
  matrix products  12.7 us (11%)
  local copies, waits for them, and re-layouts  6.68 us (6%)
    pallas_call x1, Pallas kernels, mlp_part(): pl.pallas_call(functools.partial(mlp_kernel, (n_ch, n_fb, rows)), out_sha...  81.2 us
    select_n x1, other arithmetic, attention_block(): k_full = jnp.where(slot_hit, key_new[:, None], k_cache)  8.49 us
    unnamed x10, local copies, waits for them, and re-layouts  5.17 us
    dot_general x1, matrix products, attention_block(): jnp.einsum('bkgs,bskd->bkgd', attn_prob, v_full, preferred_element_type=j...  4.01 us
    dot_general x1, matrix products, attention_block(): jnp.dot(normed, w_query, preferred_element_type=jnp.float32)  3.38 us

profile of v1, /device:TPU:113, one launch (start us, length us, event | category | flops | bytes accessed | tf_op | source)
XLA Modules:
  0.0 114.3 jit_solution(9077488772582736324)
XLA Ops:
  0.6 0.0 copy-start.1
  0.6 0.0 copy-start.2
  0.7 0.0 copy-start.3
  0.7 0.8 convert_element_type.57
  1.5 1.7 %fusion.5 = f32[128]{0:T(128)S(1)} fusion(bf16[128,5120]{1,0:T(8,128)(2,1)} %resid_ref.1), kind=kLoop, calls=%fused_computation.9 | loop fusion | flops 1965952 | bytes 1311232 | tf_op jit(solution)/shard_map/reduce_sum | solution.py:27
  3.2 0.7 convert_element_type.52
  3.9 1.3 %reshape.246.gain_ref = bf16[1,5120]{1,0:T(2,128)(2,1)} reshape(bf16[5120]{0:T(1024)(128)(2,1)} %param.22) | data formatting | bytes 20480 | tf_op jit(solution)/shard_map/reshape | solution.py:339
  5.2 2.3 %convolution_convert_fusion.1 = bf16[128,128]{1,0:T(8,128)(2,1)S(1)} fusion(bf16[5120,128]{1,0:T(8,128)(2,1)} %param.20, bf16[128,5120]{1,0:T(8,128)(2,1)} %resid_ref.1, f32[5120]{0:T(1024)S(1)} %convert_element_type.52, f32[128]{0:T(128)S(1)} %add_rsqrt_fusion), kind=kOutput, calls=%fused_computation.19 | convolution fusion | flops 170409984 | bytes 2675200 | tf_op jit(solution)/shard_map/dot_general | solution.py:63
  7.5 0.0 copy-done.2
  7.5 0.1 iota_compare_fusion.1
  7.6 0.0 copy-done.1
  7.6 0.0 copy-done.3
  7.6 0.8 fusion.21
  8.4 0.2 fusion.35
  8.6 0.1 copy.16
  8.7 0.3 multiply_cosine_fusion
  9.0 3.4 %fusion.19 = f32[128,512]{1,0:T(8,128)S(1)} fusion(bf16[5120,512]{1,0:T(8,128)(2,1)} %param.18, bf16[128,5120]{1,0:T(8,128)(2,1)S(1)} %copy-done.1, f32[5120]{0:T(1024)S(1)} %convert_element_type.52, f32[128]{0:T(128)S(1)} %add_rsqrt_fusion), kind=kOutput, calls=%fused_computation.18 | convolution fusion | flops 673841152 | bytes 6836736 | tf_op jit(solution)/shard_map/dot_general | solution.py:61
  12.4 0.1 reshape.247
  12.5 0.3 subtract_convert_fusion
  12.8 8.5 %broadcast_select_fusion.1 = (bf16[128,128,1,128]{3,1,2,0:T(8,128)(2,1)S(1)}, bf16[128,128,1,128]{3,1,2,0:T(8,128)(2,1)}) fusion(bf16[128,128,1,128]{3,1,2,0:T(8,128)(2,1)} %param.15, pred[128,128]{1,0:T(8,128)(4,1)S(1)} %get-tuple-element.12, bf16[128,128]{1,0:T(8,128)(2,1)S(1)} %copy.16, bf16[128,128,1,128]{3,1,2,0:T(8,128)(2,1)} %param.16, ...), kind=kLoop, calls=%fused_computation.6 | loop fusion | flops 4194304 | bytes 16859136 | tf_op jit(solution)/shard_map/jit(_where)/select_n | solution.py:72
  21.3 0.0 copy-start
  21.3 2.0 %copy-done = bf16[128,128,1,128]{3,1,2,0:T(8,128)(2,1)} copy-done((bf16[128,128,1,128]{3,1,2,0:T(8,128)(2,1)}, bf16[128,128,1,128]{3,1,2,0:T(8,128)(2,1)S(1)}, u32[]{:S(2)}) %copy-start) | copy-done | bytes 4194328
  23.3 2.3 %fusion.13 = f32[128,4,128]{2,1,0:T(4,128)S(1)} fusion(bf16[128,128,1,128]{3,1,2,0:T(8,128)(2,1)S(1)} %get-tuple-element.17, bf16[128,4,64]{2,1,0:T(4,128)(2,1)S(1)} %get-tuple-element.4, bf16[128,4,64]{2,1,0:T(4,128)(2,1)S(1)} %get-tuple-element.3, pred[128,128]{1,0:T(8,128)(4,1)S(1)} %get-tuple-element.11), kind=kOutput, calls=%fused_computation.15 | convolution fusion | flops 17170432 | bytes 4603904 | tf_op jit(solution)/shard_map/bkgd,bskd->bkgs/dot_general | solution.py:74
  25.6 0.4 fusion.40
  26.0 4.0 %fusion.16 = bf16[128,4,128]{2,1,0:T(4,128)(2,1)S(1)} fusion(bf16[128,128,1,128]{3,1,2,0:T(8,128)(2,1)} %get-tuple-element.18, f32[128,4]{1,0:T(8,128)S(1)} %fusion.40, f32[128,4,128]{2,1,0:T(4,128)S(1)} %fusion.13), kind=kOutput, calls=%fused_computation.16 | convolution fusion | flops 17040000 | bytes 4589568 | tf_op jit(solution)/shard_map/bkgs,bskd->bkgd/dot_general | solution.py:79
  30.0 0.7 copy.19
  30.7 81.2 %out_mlp.1 = bf16[128,5120]{1,0:T(8,128)(2,1)} custom-call(bf16[128,512]{1,0:T(8,128)(2,1)} %bitcast.30, bf16[128,5120]{1,0:T(8,128)(2,1)} %resid_ref.1, bf16[1,5120]{1,0:T(2,128)(2,1)} %reshape.246.gain_ref, bf16[512,5120]{1,0:T(8,128)(2,1)} %wo_ref.1, bf16[5120,4096]{1,0:T(8,128)(2,1)} %wg_ref.1, bf16[5120,4096]{1,0:T(8,128)(2,1)} %wu_ref.1, ...), custom_call_target="tpu_custom_call" | custom-call | flops 16106127360 | bytes 125829120 | tf_op jit(solution)/shard_map/out_mlp/pallas_call | solution.py:314
  111.8 2.5 %copy.21 = bf16[128,5120]{1,0:T(8,128)(2,1)} copy(bf16[128,5120]{1,0:T(8,128)(2,1)} %out_mlp.1) | data formatting | bytes 2621440
  (3 shorter events, 0.0 us)
Async XLA Ops:
  0.6 7.0 %copy-start.1 = (bf16[128,5120]{1,0:T(8,128)(2,1)S(1)}, bf16[128,5120]{1,0:T(8,128)(2,1)}, u32[]{:S(2)}) copy-start(bf16[128,5120]{1,0:T(8,128)(2,1)} %resid_ref.1) | copy-start | bytes 3932164
  0.6 6.8 %copy-start.2 = (s32[128]{0:T(128)S(1)}, s32[128]{0:T(128)}, u32[]{:S(2)}) copy-start(s32[128]{0:T(128)} %param.14) | copy-start | bytes 1540
  0.7 6.9 %copy-start.3 = (bf16[5120,128]{1,0:T(8,128)(2,1)S(1)}, bf16[5120,128]{1,0:T(8,128)(2,1)}, u32[]{:S(2)}) copy-start(bf16[5120,128]{1,0:T(8,128)(2,1)} %param.19) | copy-start | bytes 3932164
  21.3 2.0 %copy-start = (bf16[128,128,1,128]{3,1,2,0:T(8,128)(2,1)}, bf16[128,128,1,128]{3,1,2,0:T(8,128)(2,1)S(1)}, u32[]{:S(2)}) copy-start(bf16[128,128,1,128]{3,1,2,0:T(8,128)(2,1)S(1)} %get-tuple-element.17) | copy-start | bytes 12582916

commit v2 on v1

--- a/solution.py
+++ b/solution.py
@@ -2,6 +2,7 @@
 import math
 import jax
 import jax.numpy as jnp
+import numpy as np
 from jax import lax
 from jax.experimental import pallas as pl
 from jax.experimental.pallas import tpu as pltpu
@@ -17,68 +18,176 @@
 MESH = pl.DeviceIdType.MESH
 BLK = 512
 SLOTS = 11
+SB = 8
+UNROLL = 4
+QCH = 5
 LAG_D, LAG_1, LAG_2 = 3, 7, 11
 GLAG_2, GLAG_3 = 3, 5
 ZLAGS = (1, 3, 5, 7, 9, 11)
 
 
-def rms_norm(rows_in, gain):
-    rows_f = rows_in.astype(jnp.float32)
-    mean_sq = jnp.mean(rows_f * rows_f, axis=-1, keepdims=True)
-    return (rows_f * lax.rsqrt(mean_sq + EPS) * gain.astype(jnp.float32)).astype(jnp.bfloat16)
-
-
-def rope_tables(positions, head_dim):
-    half_dim = head_dim // 2
-    exponents = jnp.arange(half_dim, dtype=jnp.float32) * (2.0 / head_dim)
-    inv_freq = 1.0 / jnp.power(ROPE_THETA, exponents)
+def rope_freqs(head_dim):
+    exponents = np.arange(head_dim // 2) * (2.0 / head_dim)
+    inv_freq = 1.0 / np.power(ROPE_THETA, exponents)
     wavelen = (2.0 * math.pi) / inv_freq
     smooth = (ORIG_CTX / wavelen - LOW_FACTOR) / (HIGH_FACTOR - LOW_FACTOR)
     blended = (1.0 - smooth) * inv_freq / ROPE_FACTOR + smooth * inv_freq
-    inv_freq = jnp.where(wavelen < ORIG_CTX / HIGH_FACTOR, inv_freq,
-                         jnp.where(wavelen > ORIG_CTX / LOW_FACTOR, inv_freq / ROPE_FACTOR, blended))
-    angles = positions.astype(jnp.float32)[:, None] * inv_freq[None, :]
-    return jnp.cos(angles), jnp.sin(angles)
-
-
-def apply_rope(vectors, cos_t, sin_t):
-    half_dim = vectors.shape[-1] // 2
-    lower_half = vectors[..., :half_dim]
-    upper_half = vectors[..., half_dim:]
-    cos_b = cos_t[:, None, :]
-    sin_b = sin_t[:, None, :]
-    return jnp.concatenate([lower_half * cos_b - upper_half * sin_b,
-                            upper_half * cos_b + lower_half * sin_b], axis=-1)
-
-
-def attention_block(resid_in, positions, k_cache, v_cache, gain_attn, w_query, w_key, w_value):
-    n_seqs = resid_in.shape[0]
-    cache_len = k_cache.shape[1]
-    kv_heads = k_cache.shape[2]
-    head_dim = k_cache.shape[3]
-    group_size = w_query.shape[1] // (kv_heads * head_dim)
-    normed = rms_norm(resid_in, gain_attn)
-    queries = jnp.dot(normed, w_query, preferred_element_type=jnp.float32).astype(jnp.bfloat16)
-    key_new = jnp.dot(normed, w_key, preferred_element_type=jnp.float32).astype(jnp.bfloat16)
-    value_new = jnp.dot(normed, w_value, preferred_element_type=jnp.float32).astype(jnp.bfloat16)
-    cos_t, sin_t = rope_tables(positions, head_dim)
-    queries = apply_rope(queries.reshape(n_seqs, kv_heads * group_size, head_dim).astype(jnp.float32), cos_t, sin_t)
-    queries = queries.astype(jnp.bfloat16).reshape(n_seqs, kv_heads, group_size, head_dim)
-    key_new = apply_rope(key_new.reshape(n_seqs, kv_heads, head_dim).astype(jnp.float32), cos_t, sin_t)
-    key_new = key_new.astype(jnp.bfloat16)
-    value_new = value_new.reshape(n_seqs, kv_heads, head_dim)
-    slot_iota = lax.broadcasted_iota(jnp.int32, (n_seqs, cache_len), 1)
-    slot_hit = (slot_iota == positions[:, None])[:, :, None, None]
-    k_full = jnp.where(slot_hit, key_new[:, None], k_cache)
-    v_full = jnp.where(slot_hit, value_new[:, None], v_cache)
-    scores = jnp.einsum('bkgd,bskd->bkgs', queries, k_full, preferred_element_type=jnp.float32)
-    scores = scores * (1.0 / math.sqrt(head_dim))
-    valid = (slot_iota <= positions[:, None])[:, None, None, :]
-    scores = jnp.where(valid, scores, -jnp.inf)
-    attn_prob = jax.nn.softmax(scores, axis=-1).astype(jnp.bfloat16)
-    attn_out = jnp.einsum('bkgs,bskd->bkgd', attn_prob, v_full, preferred_element_type=jnp.float32)
-    attn_out = attn_out.astype(jnp.bfloat16).reshape(n_seqs, kv_heads * group_size * head_dim)
-    return attn_out, k_full, v_full
+    inv_freq = np.where(wavelen < ORIG_CTX / HIGH_FACTOR, inv_freq,
+                        np.where(wavelen > ORIG_CTX / LOW_FACTOR, inv_freq / ROPE_FACTOR, blended))
+    return np.concatenate([inv_freq, inv_freq])[None].astype(np.float32)
+
+
+def attn_kernel(pos_s, resid_ref, gain_ref, pos_ref, freq_ref, wq_ref, wk_ref, wv_ref, kc_ref, vc_ref,
+                out_ref, ko_ref, vo_ref, wq, wk, wv, kbuf, vbuf, normed, q_rot, k_rot, v_new, pos_b, o_buf,
+                q_sem, k_sem, v_sem, ko_sem, vo_sem):
+    f32, bf16 = jnp.float32, jnp.bfloat16
+    n_seqs, model = resid_ref.shape
+    cache_len, dim = kbuf.shape[1], kbuf.shape[2]
+    heads = wq.shape[1] // dim
+    n_blk = n_seqs // SB
+    kc = model // QCH
+
+    def w_copies(i):
+        sl = pl.ds(i * kc, kc)
+        return [pltpu.make_async_copy(src.at[sl], dst.at[sl], q_sem.at[i, j])
+                for j, (src, dst) in enumerate(((wq_ref, wq), (wk_ref, wk), (wv_ref, wv)))]
+
+    def seqs(i):
+        return pl.ds(pl.multiple_of(i * SB, SB), SB)
+
+    def k_in(i):
+        return pltpu.make_async_copy(kc_ref.at[seqs(i)], kbuf.at[seqs(i)], k_sem.at[i])
+
+    def v_in(i):
+        return pltpu.make_async_copy(vc_ref.at[seqs(i)], vbuf.at[seqs(i)], v_sem.at[i])
+
+    def k_out(i):
+        return pltpu.make_async_copy(kbuf.at[seqs(i)], ko_ref.at[seqs(i)], ko_sem.at[i])
+
+    def v_out(i):
+        return pltpu.make_async_copy(vbuf.at[seqs(i)], vo_ref.at[seqs(i)], vo_sem.at[i])
+
+    for i in range(QCH):
+        for c in w_copies(i):
+            c.start()
+    for i in range(n_blk):
+        k_in(i).start()
+        v_in(i).start()
+
+    row_i = lax.broadcasted_iota(jnp.int32, (n_seqs, n_seqs), 0)
+    col_i = lax.broadcasted_iota(jnp.int32, (n_seqs, n_seqs), 1)
+    pos_f = pos_ref[...].astype(f32)
+    pos_col = jnp.sum(jnp.where(row_i == col_i, pos_f, 0.0), axis=1, keepdims=True)
+    pos_b[...] = jnp.broadcast_to(pos_col, pos_b.shape)
+    angles = pos_b[...] * freq_ref[...]
+    cos_t = jnp.cos(angles)
+    lane = lax.broadcasted_iota(jnp.int32, angles.shape, 1)
+    sin_t = jnp.sin(angles)
+    sin_t = jnp.where(lane < dim // 2, -sin_t, sin_t)
+
+    total = jnp.zeros((n_seqs, 1), f32)
+    for i in range(QCH):
+        x = resid_ref[:, i * kc:(i + 1) * kc].astype(f32)
+        total += jnp.sum(x * x, axis=-1, keepdims=True)
+    inv = lax.rsqrt(total * (1.0 / model) + EPS)
+    for i in range(QCH):
+        sl = slice(i * kc, (i + 1) * kc)
+        normed[:, sl] = (resid_ref[:, sl].astype(f32) * inv * gain_ref[:, sl].astype(f32)).astype(bf16)
+
+    q = k = v = None
+    for i in range(QCH):
+        for c in w_copies(i):
+            c.wait()
+        sl = slice(i * kc, (i + 1) * kc)
+        h = normed[:, sl]
+        parts = [jnp.dot(h, w[sl, :], preferred_element_type=f32) for w in (wq, wk, wv)]
+        q, k, v = parts if q is None else [x + y for x, y in zip((q, k, v), parts)]
+
+    def rope(x):
+        x = x.astype(bf16).astype(f32)
+        return (x * cos_t + pltpu.roll(x, dim // 2, 1) * sin_t).astype(bf16).astype(f32)
+
+    for j in range(heads):
+        q_rot[j] = rope(q[:, j * dim:(j + 1) * dim])
+    k_rot[...] = rope(k)
+    v_new[...] = v.astype(bf16).astype(f32)
+
+    rows, cols = heads * SB, SB * cache_len
+    r_i = lax.broadcasted_iota(jnp.int32, (rows, cols), 0)
+    c_i = lax.broadcasted_iota(jnp.int32, (rows, cols), 1)
+    slot_of = jnp.where(lax.rem(r_i, SB) == c_i // cache_len, lax.rem(c_i, cache_len), 2 * cache_len).astype(f32)
+    slot_row = lax.broadcasted_iota(jnp.int32, (cache_len, dim), 0)
+    scale = 1.0 / math.sqrt(dim)
+
+    def block(i):
+        k_in(i).wait()
+        v_in(i).wait()
+        for s in range(SB):
+            n = i * SB + s
+            hit = slot_row == pos_s[n]
+            kbuf[n] = jnp.where(hit, k_rot[pl.ds(n, 1), :], kbuf[n].astype(f32)).astype(bf16)
+            vbuf[n] = jnp.where(hit, v_new[pl.ds(n, 1), :], vbuf[n].astype(f32)).astype(bf16)
+        k_out(i).start()
+        v_out(i).start()
+        q_b = jnp.concatenate([q_rot[j, seqs(i), :] for j in range(heads)], axis=0).astype(bf16)
+        k_b = kbuf[seqs(i)].reshape(cols, dim)
+        v_b = vbuf[seqs(i)].reshape(cols, dim)
+        sc = lax.dot_general(q_b, k_b, (((1,), (1,)), ((), ())), preferred_element_type=f32) * scale
+        p_b = jnp.concatenate([pos_b[seqs(i), :]] * heads, axis=0)
+        p_b = jnp.concatenate([p_b] * SB, axis=1)
+        sc = jnp.where(slot_of <= p_b, sc, -jnp.inf)
+        ex = jnp.exp(sc - jnp.max(sc, axis=-1, keepdims=True))
+        prob = (ex * (1.0 / jnp.sum(ex, axis=-1, keepdims=True))).astype(bf16)
+        o = jnp.dot(prob, v_b, preferred_element_type=f32)
+        for j in range(heads):
+            o_buf[seqs(i), j * dim:(j + 1) * dim] = o[j * SB:(j + 1) * SB]
+
+    def step(g, c):
+        for r in range(UNROLL):
+            block(g * UNROLL + r)
+        return c
+    lax.fori_loop(0, n_blk // UNROLL, step, 0)
+    out_ref[...] = o_buf[...].astype(bf16)
+
+    def finish(i, c):
+        k_out(i).wait()
+        v_out(i).wait()
+        return c
+    lax.fori_loop(0, n_blk, finish, 0)
+
+
+def attention_part(resid_in, positions, k_cache, v_cache, gain_attn, w_query, w_key, w_value):
+    n_seqs, model = resid_in.shape
+    cache_len, kv_heads, dim = k_cache.shape[1:]
+    q_width = w_query.shape[1]
+    f32, bf16 = jnp.float32, jnp.bfloat16
+    cache_flat = (n_seqs, cache_len * kv_heads, dim)
+    hbm = pl.BlockSpec(memory_space=pltpu.HBM)
+    vmem = pl.BlockSpec(memory_space=pltpu.VMEM)
+    smem = pl.BlockSpec(memory_space=pltpu.SMEM)
+    n_blk = n_seqs // SB
+    out, k_full, v_full = pl.pallas_call(
+        attn_kernel,
+        out_shape=(jax.ShapeDtypeStruct((n_seqs, q_width), bf16), jax.ShapeDtypeStruct(cache_flat, bf16),
+                   jax.ShapeDtypeStruct(cache_flat, bf16)),
+        in_specs=[smem, vmem, vmem, vmem, vmem, hbm, hbm, hbm, hbm, hbm],
+        out_specs=(vmem, hbm, hbm),
+        scratch_shapes=[
+            pltpu.VMEM(w_query.shape, bf16), pltpu.VMEM(w_key.shape, bf16), pltpu.VMEM(w_value.shape, bf16),
+            pltpu.VMEM(cache_flat, bf16), pltpu.VMEM(cache_flat, bf16),
+            pltpu.VMEM((n_seqs, model), bf16), pltpu.VMEM((q_width // dim, n_seqs, dim), f32),
+            pltpu.VMEM((n_seqs, dim), f32), pltpu.VMEM((n_seqs, dim), f32), pltpu.VMEM((n_seqs, dim), f32),
+            pltpu.VMEM((n_seqs, q_width), f32),
+            pltpu.SemaphoreType.DMA((QCH, 3)),
+            pltpu.SemaphoreType.DMA((n_blk,)), pltpu.SemaphoreType.DMA((n_blk,)),
+            pltpu.SemaphoreType.DMA((n_blk,)), pltpu.SemaphoreType.DMA((n_blk,)),
+        ],
+        compiler_params=pltpu.CompilerParams(vmem_limit_bytes=60_000_000),
+        cost_estimate=pl.CostEstimate(flops=2 * n_seqs * model * q_width, bytes_accessed=30_000_000, transcendentals=0),
+        name='attn',
+    )(positions, resid_in, gain_attn.reshape(1, model), positions.reshape(1, n_seqs), rope_freqs(dim),
+      w_query, w_key, w_value, k_cache.reshape(cache_flat), v_cache.reshape(cache_flat))
+    return out, k_full.reshape(k_cache.shape), v_full.reshape(v_cache.shape)
 
 
 def mlp_kernel(dims, o_ref, resid_ref, gain_ref, wo_ref, wg_ref, wu_ref, wd_ref, out_ref,
@@ -342,8 +451,8 @@
 def solution(mesh):
     def layer_local(resid_in, positions, k_cache, v_cache, gain_attn, w_query, w_key, w_value,
                     w_out, gain_mlp, w_gate, w_up, w_down):
-        attn_out, k_full, v_full = attention_block(resid_in, positions, k_cache, v_cache,
-                                                   gain_attn, w_query, w_key, w_value)
+        attn_out, k_full, v_full = attention_part(resid_in, positions, k_cache, v_cache,
+                                                  gain_attn, w_query, w_key, w_value)
         resid_out = mlp_part(attn_out, resid_in, gain_mlp, w_out, w_gate, w_up, w_down)
         return resid_out, k_full, v_full
 

time: 115 us -> 106 us (0.922)
  Pallas kernels: 81.2 us -> 99.8 us
  other arithmetic: 13 us -> 0 us
  matrix products: 12.7 us -> 0 us
  local copies, waits for them, and re-layouts: 6.68 us -> 5.09 us
    pallas_call x0 -> x1, Pallas kernels: none -> 18.6 us  [attention_part(): pl.pallas_call(attn_kernel, out_shape=(jax.ShapeDtypeStruct((n_seqs, q_wi...]
    dot_general x5 -> x0, matrix products: 12.7 us -> none  [the longest x1 4.01 us: attention_block(): jnp.einsum('bkgs,bskd->bkgd', attn_prob, v_full, preferred_element_type=j...]
    select_n x2 -> x0, other arithmetic: 8.51 us -> none  [the longest x1 8.49 us: attention_block(): k_full = jnp.where(slot_hit, key_new[:, None], k_cache)]
    unnamed x10 -> x1, local copies, waits for them, and re-layouts: 5.17 us -> 2.46 us
    reduce_sum x1 -> x0, other arithmetic: 1.65 us -> none  [rms_norm(): mean_sq = jnp.mean(rows_f * rows_f, axis=-1, keepdims=True)]
    convert_element_type x2 -> x0, other arithmetic: 1.52 us -> none  [the longest x1 0.81 us: rope_tables(): angles = positions.astype(jnp.float32)[:, None] * inv_freq[None, :]]
    reshape x0 -> x1, local copies, waits for them, and re-layouts: none -> 1.32 us  [attention_part(): gain_attn.reshape(1, model)]
where the time goes in v2:
time: 106 us
  Pallas kernels  99.8 us (94%)
  local copies, waits for them, and re-layouts  5.09 us (5%)
    pallas_call x1, Pallas kernels, mlp_part(): pl.pallas_call(functools.partial(mlp_kernel, (n_ch, n_fb, rows)), out_sha...  81.2 us
    pallas_call x1, Pallas kernels, attention_part(): pl.pallas_call(attn_kernel, out_shape=(jax.ShapeDtypeStruct((n_seqs, q_wi...  18.6 us
    unnamed x1, local copies, waits for them, and re-layouts  2.46 us

profile of v2, /device:TPU:113, one launch (start us, length us, event | category | flops | bytes accessed | tf_op | source)
XLA Modules:
  0.0 105.5 jit_solution(3803229156775507568)
XLA Ops:
  0.6 1.3 %reshape.27.gain_ref = bf16[1,5120]{1,0:T(2,128)(2,1)} reshape(bf16[5120]{0:T(1024)(128)(2,1)} %param.18) | data formatting | bytes 20480 | tf_op jit(solution)/shard_map/reshape | solution.py:188
  1.9 1.3 %reshape.31.gain_ref = bf16[1,5120]{1,0:T(2,128)(2,1)} reshape(bf16[5120]{0:T(1024)(128)(2,1)} %param.23) | data formatting | bytes 20480 | tf_op jit(solution)/shard_map/reshape | solution.py:448
  3.3 18.6 %attn.1 = (bf16[128,512]{1,0:T(8,128)(2,1)}, bf16[128,128,128]{2,1,0:T(8,128)(2,1)}, bf16[128,128,128]{2,1,0:T(8,128)(2,1)}) custom-call(s32[128]{0:T(128)} %pos_s.1, bf16[128,5120]{1,0:T(8,128)(2,1)} %resid_ref.3, bf16[1,5120]{1,0:T(2,128)(2,1)} %reshape.27.gain_ref, s32[1,128]{1,0:T(1,128)} %bitcast.11, f32[1,128]{1,0:T(1,128)} %constant.2.clone.freq_ref, ...), custom_call_target="tpu_custom_call" | custom-call | flops 671088640 | bytes 30000000 | tf_op jit(solution)/shard_map/attn/pallas_call | solution.py:169
  21.9 81.2 %out_mlp.1 = bf16[128,5120]{1,0:T(8,128)(2,1)} custom-call(bf16[128,512]{1,0:T(8,128)(2,1)} %get-tuple-element.6.o_ref, bf16[128,5120]{1,0:T(8,128)(2,1)} %resid_ref.3, bf16[1,5120]{1,0:T(2,128)(2,1)} %reshape.31.gain_ref, bf16[512,5120]{1,0:T(8,128)(2,1)} %wo_ref.1, bf16[5120,4096]{1,0:T(8,128)(2,1)} %wg_ref.1, bf16[5120,4096]{1,0:T(8,128)(2,1)} %wu_ref.1, ...), custom_call_target="tpu_custom_call" | custom-call | flops 16106127360 | bytes 125829120 | tf_op jit(solution)/shard_map/out_mlp/pallas_call | solution.py:423
  103.1 2.5 %copy.20 = bf16[128,5120]{1,0:T(8,128)(2,1)} copy(bf16[128,5120]{1,0:T(8,128)(2,1)} %out_mlp.1) | data formatting | bytes 2621440

commit v3 on v2

--- a/solution.py
+++ b/solution.py
@@ -21,9 +21,9 @@
 SB = 8
 UNROLL = 4
 QCH = 5
-LAG_D, LAG_1, LAG_2 = 3, 7, 11
-GLAG_2, GLAG_3 = 3, 5
-ZLAGS = (1, 3, 5, 7, 9, 11)
+LAG_D, LAG_1, LAG_2 = 2, 7, 17
+GLAG_2, GLAG_3 = 3, 4
+ZLAGS = (2, 6, 10, 14, 19, 21)
 
 
 def rope_freqs(head_dim):
@@ -37,20 +37,21 @@
     return np.concatenate([inv_freq, inv_freq])[None].astype(np.float32)
 
 
-def attn_kernel(pos_s, resid_ref, gain_ref, pos_ref, freq_ref, wq_ref, wk_ref, wv_ref, kc_ref, vc_ref,
-                out_ref, ko_ref, vo_ref, wq, wk, wv, kbuf, vbuf, normed, q_rot, k_rot, v_new, pos_b, o_buf,
-                q_sem, k_sem, v_sem, ko_sem, vo_sem):
+def attn_kernel(pos_s, resid_hbm, gain_ref, pos_ref, freq_ref, wq_ref, wk_ref, wv_ref, kc_ref, vc_ref,
+                out_ref, ko_ref, vo_ref, resid_ref, wqkv, kbuf, vbuf, normed, q_rot, k_rot, v_new, pos_b, o_buf,
+                r_sem, q_sem, k_sem, v_sem, ko_sem, vo_sem):
     f32, bf16 = jnp.float32, jnp.bfloat16
     n_seqs, model = resid_ref.shape
     cache_len, dim = kbuf.shape[1], kbuf.shape[2]
-    heads = wq.shape[1] // dim
+    heads = wq_ref.shape[1] // dim
+    width = heads * dim
     n_blk = n_seqs // SB
     kc = model // QCH
 
     def w_copies(i):
         sl = pl.ds(i * kc, kc)
-        return [pltpu.make_async_copy(src.at[sl], dst.at[sl], q_sem.at[i, j])
-                for j, (src, dst) in enumerate(((wq_ref, wq), (wk_ref, wk), (wv_ref, wv)))]
+        return [pltpu.make_async_copy(src.at[sl], wqkv.at[sl, pl.ds(at, size)], q_sem.at[i, j])
+                for j, (src, at, size) in enumerate(((wq_ref, 0, width), (wk_ref, width, dim), (wv_ref, width + dim, dim)))]
 
     def seqs(i):
         return pl.ds(pl.multiple_of(i * SB, SB), SB)
@@ -67,12 +68,10 @@
     def v_out(i):
         return pltpu.make_async_copy(vbuf.at[seqs(i)], vo_ref.at[seqs(i)], vo_sem.at[i])
 
-    for i in range(QCH):
-        for c in w_copies(i):
-            c.start()
-    for i in range(n_blk):
-        k_in(i).start()
-        v_in(i).start()
+    resid_copy = pltpu.make_async_copy(resid_hbm, resid_ref, r_sem)
+    resid_copy.start()
+    for c in w_copies(0) + w_copies(1):
+        c.start()
 
     row_i = lax.broadcasted_iota(jnp.int32, (n_seqs, n_seqs), 0)
     col_i = lax.broadcasted_iota(jnp.int32, (n_seqs, n_seqs), 1)
@@ -85,6 +84,13 @@
     sin_t = jnp.sin(angles)
     sin_t = jnp.where(lane < dim // 2, -sin_t, sin_t)
 
+    resid_copy.wait()
+    for i in range(2, QCH):
+        for c in w_copies(i):
+            c.start()
+    for i in range(n_blk):
+        k_in(i).start()
+        v_in(i).start()
     total = jnp.zeros((n_seqs, 1), f32)
     for i in range(QCH):
         x = resid_ref[:, i * kc:(i + 1) * kc].astype(f32)
@@ -92,53 +98,59 @@
     inv = lax.rsqrt(total * (1.0 / model) + EPS)
     for i in range(QCH):
         sl = slice(i * kc, (i + 1) * kc)
-        normed[:, sl] = (resid_ref[:, sl].astype(f32) * inv * gain_ref[:, sl].astype(f32)).astype(bf16)
-
-    q = k = v = None
+        normed[:, sl] = (resid_ref[:, sl].astype(f32) * inv * gain_ref[sl].astype(f32)[None]).astype(bf16)
+
+    qkv = None
     for i in range(QCH):
         for c in w_copies(i):
             c.wait()
         sl = slice(i * kc, (i + 1) * kc)
-        h = normed[:, sl]
-        parts = [jnp.dot(h, w[sl, :], preferred_element_type=f32) for w in (wq, wk, wv)]
-        q, k, v = parts if q is None else [x + y for x, y in zip((q, k, v), parts)]
+        part = jnp.dot(normed[:, sl], wqkv[sl, :], preferred_element_type=f32)
+        qkv = part if qkv is None else qkv + part
 
     def rope(x):
         x = x.astype(bf16).astype(f32)
         return (x * cos_t + pltpu.roll(x, dim // 2, 1) * sin_t).astype(bf16).astype(f32)
 
     for j in range(heads):
-        q_rot[j] = rope(q[:, j * dim:(j + 1) * dim])
-    k_rot[...] = rope(k)
-    v_new[...] = v.astype(bf16).astype(f32)
-
-    rows, cols = heads * SB, SB * cache_len
-    r_i = lax.broadcasted_iota(jnp.int32, (rows, cols), 0)
+        q_rot[j] = rope(qkv[:, j * dim:(j + 1) * dim])
+    k_rot[...] = rope(qkv[:, width:width + dim])
+    v_new[...] = qkv[:, width + dim:].astype(bf16).astype(f32)
+
+    pair = SB // 2
+    rows, cols = heads * SB, pair * cache_len
+    r_i = lax.rem(lax.broadcasted_iota(jnp.int32, (rows, cols), 0), SB)
     c_i = lax.broadcasted_iota(jnp.int32, (rows, cols), 1)
-    slot_of = jnp.where(lax.rem(r_i, SB) == c_i // cache_len, lax.rem(c_i, cache_len), 2 * cache_len).astype(f32)
-    slot_row = lax.broadcasted_iota(jnp.int32, (cache_len, dim), 0)
+    slot_of = jnp.where(lax.rem(r_i, pair) == c_i // cache_len, lax.rem(c_i, cache_len), 2 * cache_len).astype(f32)
+    early = lax.rem(lax.broadcasted_iota(jnp.int32, (rows, dim), 0), SB) < pair
+    slot_row = lax.broadcasted_iota(jnp.int32, (cache_len, dim), 0).astype(f32).astype(bf16)
     scale = 1.0 / math.sqrt(dim)
+
+    def both(buf, i):
+        first = buf[pl.ds(pl.multiple_of(i * SB, pair), pair)].reshape(cols, dim)
+        second = buf[pl.ds(pl.multiple_of(i * SB + pair, pair), pair)].reshape(cols, dim)
+        return jnp.concatenate([first, second], axis=1)
 
     def block(i):
         k_in(i).wait()
         v_in(i).wait()
         for s in range(SB):
             n = i * SB + s
-            hit = slot_row == pos_s[n]
-            kbuf[n] = jnp.where(hit, k_rot[pl.ds(n, 1), :], kbuf[n].astype(f32)).astype(bf16)
-            vbuf[n] = jnp.where(hit, v_new[pl.ds(n, 1), :], vbuf[n].astype(f32)).astype(bf16)
+            hit = slot_row == jnp.full((cache_len, dim), pos_s[n].astype(f32)).astype(bf16)
+            kbuf[n] = jnp.where(hit, jnp.broadcast_to(k_rot[pl.ds(n, 1), :], (cache_len, dim)).astype(bf16), kbuf[n])
+            vbuf[n] = jnp.where(hit, jnp.broadcast_to(v_new[pl.ds(n, 1), :], (cache_len, dim)).astype(bf16), vbuf[n])
         k_out(i).start()
         v_out(i).start()
-        q_b = jnp.concatenate([q_rot[j, seqs(i), :] for j in range(heads)], axis=0).astype(bf16)
-        k_b = kbuf[seqs(i)].reshape(cols, dim)
-        v_b = vbuf[seqs(i)].reshape(cols, dim)
-        sc = lax.dot_general(q_b, k_b, (((1,), (1,)), ((), ())), preferred_element_type=f32) * scale
+        q_b = jnp.concatenate([q_rot[j, seqs(i), :] for j in range(heads)], axis=0)
+        q_b = jnp.concatenate([jnp.where(early, q_b, 0.0), jnp.where(early, 0.0, q_b)], axis=1).astype(bf16)
+        sc = lax.dot_general(q_b, both(kbuf, i), (((1,), (1,)), ((), ())), preferred_element_type=f32) * scale
         p_b = jnp.concatenate([pos_b[seqs(i), :]] * heads, axis=0)
-        p_b = jnp.concatenate([p_b] * SB, axis=1)
+        p_b = jnp.concatenate([p_b] * pair, axis=1)
         sc = jnp.where(slot_of <= p_b, sc, -jnp.inf)
         ex = jnp.exp(sc - jnp.max(sc, axis=-1, keepdims=True))
         prob = (ex * (1.0 / jnp.sum(ex, axis=-1, keepdims=True))).astype(bf16)
-        o = jnp.dot(prob, v_b, preferred_element_type=f32)
+        o = jnp.dot(prob, both(vbuf, i), preferred_element_type=f32)
+        o = jnp.where(early, o[:, :dim], o[:, dim:])
         for j in range(heads):
             o_buf[seqs(i), j * dim:(j + 1) * dim] = o[j * SB:(j + 1) * SB]
 
@@ -168,24 +180,24 @@
     n_blk = n_seqs // SB
     out, k_full, v_full = pl.pallas_call(
         attn_kernel,
-        out_shape=(jax.ShapeDtypeStruct((n_seqs, q_width), bf16), jax.ShapeDtypeStruct(cache_flat, bf16),
+        out_shape=(pltpu.VMEM((n_seqs, q_width), bf16), jax.ShapeDtypeStruct(cache_flat, bf16),
                    jax.ShapeDtypeStruct(cache_flat, bf16)),
-        in_specs=[smem, vmem, vmem, vmem, vmem, hbm, hbm, hbm, hbm, hbm],
+        in_specs=[smem, hbm, vmem, vmem, vmem, hbm, hbm, hbm, hbm, hbm],
         out_specs=(vmem, hbm, hbm),
         scratch_shapes=[
-            pltpu.VMEM(w_query.shape, bf16), pltpu.VMEM(w_key.shape, bf16), pltpu.VMEM(w_value.shape, bf16),
+            pltpu.VMEM((n_seqs, model), bf16), pltpu.VMEM((model, q_width + 2 * dim), bf16),
             pltpu.VMEM(cache_flat, bf16), pltpu.VMEM(cache_flat, bf16),
             pltpu.VMEM((n_seqs, model), bf16), pltpu.VMEM((q_width // dim, n_seqs, dim), f32),
             pltpu.VMEM((n_seqs, dim), f32), pltpu.VMEM((n_seqs, dim), f32), pltpu.VMEM((n_seqs, dim), f32),
             pltpu.VMEM((n_seqs, q_width), f32),
-            pltpu.SemaphoreType.DMA((QCH, 3)),
+            pltpu.SemaphoreType.DMA, pltpu.SemaphoreType.DMA((QCH, 3)),
             pltpu.SemaphoreType.DMA((n_blk,)), pltpu.SemaphoreType.DMA((n_blk,)),
             pltpu.SemaphoreType.DMA((n_blk,)), pltpu.SemaphoreType.DMA((n_blk,)),
         ],
         compiler_params=pltpu.CompilerParams(vmem_limit_bytes=60_000_000),
         cost_estimate=pl.CostEstimate(flops=2 * n_seqs * model * q_width, bytes_accessed=30_000_000, transcendentals=0),
         name='attn',
-    )(positions, resid_in, gain_attn.reshape(1, model), positions.reshape(1, n_seqs), rope_freqs(dim),
+    )(positions, resid_in, gain_attn, positions.reshape(1, n_seqs), rope_freqs(dim),
       w_query, w_key, w_value, k_cache.reshape(cache_flat), v_cache.reshape(cache_flat))
     return out, k_full.reshape(k_cache.shape), v_full.reshape(v_cache.shape)
 
@@ -334,7 +346,7 @@
         total += jnp.sum(x1 * x1, axis=-1, keepdims=True)
     inv = lax.rsqrt(total * (1.0 / (n_ch * BLK)) + EPS)
     for u in range(n_ch):
-        gain = gain_ref[:, u * BLK:(u + 1) * BLK].astype(jnp.float32)
+        gain = gain_ref[u * BLK:(u + 1) * BLK].astype(jnp.float32)[None]
         hbuf[u, own] = (x_own[u] * inv * gain).astype(jnp.bfloat16).astype(jnp.float32)
         g_1(u).start()
 
@@ -422,7 +434,7 @@
     vmem_spec = pl.BlockSpec(memory_space=pltpu.VMEM)
     return pl.pallas_call(
         functools.partial(mlp_kernel, (n_ch, n_fb, rows)),
-        out_shape=jax.ShapeDtypeStruct((n_seqs, model), bf16),
+        out_shape=pltpu.VMEM((n_seqs, model), bf16),
         in_specs=[vmem_spec, any_spec, vmem_spec, any_spec, any_spec, any_spec, any_spec],
         out_specs=vmem_spec,
         scratch_shapes=[
@@ -442,10 +454,10 @@
             pltpu.SemaphoreType.DMA((6, n_ch)),
             pltpu.SemaphoreType.DMA((6, n_ch)),
         ],
-        compiler_params=pltpu.CompilerParams(collective_id=0, has_side_effects=True, vmem_limit_bytes=66_900_000),
+        compiler_params=pltpu.CompilerParams(collective_id=0, has_side_effects=True, vmem_limit_bytes=61_500_000),
         cost_estimate=pl.CostEstimate(flops=6 * n_seqs * model * ffn, bytes_accessed=6 * model * ffn, transcendentals=0),
         name='out_mlp',
-    )(attn_out, resid_in, gain_mlp.reshape(1, model), w_out, w_gate, w_up, w_down)
+    )(attn_out, resid_in, gain_mlp, w_out, w_gate, w_up, w_down)
 
 
 def solution(mesh):

time: 106 us -> 97.7 us (0.922)
  Pallas kernels: 99.8 us -> 95.2 us
  local copies, waits for them, and re-layouts: 5.09 us -> 1.71 us
    pallas_call x1, Pallas kernels: 81.2 us -> 77 us  [mlp_part(): pl.pallas_call(functools.partial(mlp_kernel, (n_ch, n_fb, rows)), out_sha...]
    reshape x2 -> x0, local copies, waits for them, and re-layouts: 2.63 us -> none  [the longest x1 1.32 us: attention_part(): gain_attn.reshape(1, model)]
    unnamed x1 -> x3, local copies, waits for them, and re-layouts: 2.46 us -> 1.71 us
where the time goes in v3:
time: 97.7 us; the launch traced here: 97.6 us
  Pallas kernels  95.2 us (97%)
  local copies, waits for them, and re-layouts  1.71 us (2%)
    pallas_call x1, Pallas kernels, mlp_part(): pl.pallas_call(functools.partial(mlp_kernel, (n_ch, n_fb, rows)), out_sha...  77 us
    pallas_call x1, Pallas kernels, attention_part(): pl.pallas_call(attn_kernel, out_shape=(pltpu.VMEM((n_seqs, q_width), bf16...  18.2 us

profile of v3, /device:TPU:113, one launch (start us, length us, event | category | flops | bytes accessed | tf_op | source)
XLA Modules:
  0.0 97.6 jit_solution(14493655173556597913)
XLA Ops:
  0.6 18.2 %attn.1 = (bf16[128,512]{1,0:T(8,128)(2,1)S(1)}, bf16[128,128,128]{2,1,0:T(8,128)(2,1)}, bf16[128,128,128]{2,1,0:T(8,128)(2,1)}) custom-call(s32[128]{0:T(128)} %pos_s.1, bf16[128,5120]{1,0:T(8,128)(2,1)} %resid_ref.1, bf16[5120]{0:T(1024)(128)(2,1)} %gain_ref.2, s32[1,128]{1,0:T(1,128)} %bitcast.11, f32[1,128]{1,0:T(1,128)} %constant.2.clone.freq_ref, ...), custom_call_target="tpu_custom_call" | custom-call | flops 671088640 | bytes 30000000 | tf_op jit(solution)/shard_map/attn/pallas_call | solution.py:181
  18.8 0.0 copy-start
  18.8 0.6 copy-done
  19.5 77.0 %out_mlp.1 = bf16[128,5120]{1,0:T(8,128)(2,1)S(1)} custom-call(bf16[128,512]{1,0:T(8,128)(2,1)} %copy-done, bf16[128,5120]{1,0:T(8,128)(2,1)} %resid_ref.1, bf16[5120]{0:T(1024)(128)(2,1)} %gain_ref.3, bf16[512,5120]{1,0:T(8,128)(2,1)} %wo_ref.1, bf16[5120,4096]{1,0:T(8,128)(2,1)} %wg_ref.1, bf16[5120,4096]{1,0:T(8,128)(2,1)} %wu_ref.1, ...), custom_call_target="tpu_custom_call" | custom-call | flops 16106127360 | bytes 125829120 | tf_op jit(solution)/shard_map/out_mlp/pallas_call | solution.py:435
  96.5 1.1 %copy.20 = bf16[128,5120]{1,0:T(8,128)(2,1)} copy(bf16[128,5120]{1,0:T(8,128)(2,1)S(1)} %out_mlp.1) | data formatting | bytes 2621440
Async XLA Ops:
  18.8 0.7 copy-start

commit v4 on v3

--- a/solution.py
+++ b/solution.py
@@ -17,7 +17,7 @@
 
 MESH = pl.DeviceIdType.MESH
 BLK = 512
-SLOTS = 11
+SLOTS = 12
 SB = 8
 UNROLL = 4
 QCH = 5
@@ -88,7 +88,7 @@
     for i in range(2, QCH):
         for c in w_copies(i):
             c.start()
-    for i in range(n_blk):
+    for i in range(UNROLL):
         k_in(i).start()
         v_in(i).start()
     total = jnp.zeros((n_seqs, 1), f32)
@@ -100,6 +100,10 @@
         sl = slice(i * kc, (i + 1) * kc)
         normed[:, sl] = (resid_ref[:, sl].astype(f32) * inv * gain_ref[sl].astype(f32)[None]).astype(bf16)
 
+    for i in range(UNROLL, n_blk):
+        k_in(i).start()
+        v_in(i).start()
+
     qkv = None
     for i in range(QCH):
         for c in w_copies(i):
@@ -131,32 +135,41 @@
         second = buf[pl.ds(pl.multiple_of(i * SB + pair, pair), pair)].reshape(cols, dim)
         return jnp.concatenate([first, second], axis=1)
 
-    def block(i):
-        k_in(i).wait()
-        v_in(i).wait()
+    def update(i):
         for s in range(SB):
             n = i * SB + s
             hit = slot_row == jnp.full((cache_len, dim), pos_s[n].astype(f32)).astype(bf16)
             kbuf[n] = jnp.where(hit, jnp.broadcast_to(k_rot[pl.ds(n, 1), :], (cache_len, dim)).astype(bf16), kbuf[n])
             vbuf[n] = jnp.where(hit, jnp.broadcast_to(v_new[pl.ds(n, 1), :], (cache_len, dim)).astype(bf16), vbuf[n])
-        k_out(i).start()
-        v_out(i).start()
+
+    def scores(i):
         q_b = jnp.concatenate([q_rot[j, seqs(i), :] for j in range(heads)], axis=0)
         q_b = jnp.concatenate([jnp.where(early, q_b, 0.0), jnp.where(early, 0.0, q_b)], axis=1).astype(bf16)
-        sc = lax.dot_general(q_b, both(kbuf, i), (((1,), (1,)), ((), ())), preferred_element_type=f32) * scale
+        return lax.dot_general(q_b, both(kbuf, i), (((1,), (1,)), ((), ())), preferred_element_type=f32) * scale
+
+    def softmax(i, sc):
         p_b = jnp.concatenate([pos_b[seqs(i), :]] * heads, axis=0)
         p_b = jnp.concatenate([p_b] * pair, axis=1)
         sc = jnp.where(slot_of <= p_b, sc, -jnp.inf)
         ex = jnp.exp(sc - jnp.max(sc, axis=-1, keepdims=True))
-        prob = (ex * (1.0 / jnp.sum(ex, axis=-1, keepdims=True))).astype(bf16)
-        o = jnp.dot(prob, both(vbuf, i), preferred_element_type=f32)
-        o = jnp.where(early, o[:, :dim], o[:, dim:])
-        for j in range(heads):
-            o_buf[seqs(i), j * dim:(j + 1) * dim] = o[j * SB:(j + 1) * SB]
+        return (ex * (1.0 / jnp.sum(ex, axis=-1, keepdims=True))).astype(bf16)
 
     def step(g, c):
-        for r in range(UNROLL):
-            block(g * UNROLL + r)
+        blocks = [g * UNROLL + r for r in range(UNROLL)]
+        for i in blocks:
+            k_in(i).wait()
+            v_in(i).wait()
+        for i in blocks:
+            update(i)
+        for i in blocks:
+            k_out(i).start()
+            v_out(i).start()
+        probs = [softmax(i, sc) for i, sc in [(i, scores(i)) for i in blocks]]
+        outs = [jnp.dot(prob, both(vbuf, i), preferred_element_type=f32) for i, prob in zip(blocks, probs)]
+        for i, o in zip(blocks, outs):
+            o = jnp.where(early, o[:, :dim], o[:, dim:])
+            for j in range(heads):
+                o_buf[seqs(i), j * dim:(j + 1) * dim] = o[j * SB:(j + 1) * SB]
         return c
     lax.fori_loop(0, n_blk // UNROLL, step, 0)
     out_ref[...] = o_buf[...].astype(bf16)
@@ -368,11 +381,11 @@
             g_3(u).wait_recv()
             h_k = hbuf[u].reshape(8 * rows, BLK).astype(jnp.bfloat16)
             for which, acc in ((0, acc_g), (1, acc_u)):
-                load = 2 + 2 * u + which
-                slot = wait_load(load)
+                slot = wait_load(2 + 2 * u + which)
                 for b in range(n_fb):
                     acc[b] += jnp.dot(h_k, ring[slot, b], preferred_element_type=jnp.float32)
-                issue(load + SLOTS)
+            issue(2 + 2 * u + SLOTS)
+            issue(3 + 2 * u + SLOTS)
         at(t, GLAG_3, compute)
         return c
     lax.fori_loop(0, n_ch + GLAG_3, step_g, 0)
@@ -454,7 +467,7 @@
             pltpu.SemaphoreType.DMA((6, n_ch)),
             pltpu.SemaphoreType.DMA((6, n_ch)),
         ],
-        compiler_params=pltpu.CompilerParams(collective_id=0, has_side_effects=True, vmem_limit_bytes=61_500_000),
+        compiler_params=pltpu.CompilerParams(collective_id=0, has_side_effects=True, vmem_limit_bytes=64_600_000),
         cost_estimate=pl.CostEstimate(flops=6 * n_seqs * model * ffn, bytes_accessed=6 * model * ffn, transcendentals=0),
         name='out_mlp',
     )(attn_out, resid_in, gain_mlp, w_out, w_gate, w_up, w_down)
@@ -465,6 +478,7 @@
                     w_out, gain_mlp, w_gate, w_up, w_down):
         attn_out, k_full, v_full = attention_part(resid_in, positions, k_cache, v_cache,
                                                   gain_attn, w_query, w_key, w_value)
+        attn_out = pltpu.with_memory_space_constraint(attn_out, pltpu.VMEM)
         resid_out = mlp_part(attn_out, resid_in, gain_mlp, w_out, w_gate, w_up, w_down)
         return resid_out, k_full, v_full
 

time: 97.7 us -> 91.7 us (0.939)
  Pallas kernels: 95.2 us -> 89.8 us
    pallas_call x1, Pallas kernels: 18.2 us -> 13.4 us  [attention_part(): pl.pallas_call(attn_kernel, out_shape=(pltpu.VMEM((n_seqs, q_width), bf16...]
where the time goes in v4:
time: 91.7 us; the launch traced here: 91.5 us
  Pallas kernels  89.8 us (98%)
  local copies, waits for them, and re-layouts  1.06 us (1%)
    pallas_call x1, Pallas kernels, mlp_part(): pl.pallas_call(functools.partial(mlp_kernel, (n_ch, n_fb, rows)), out_sha...  76.4 us
    pallas_call x1, Pallas kernels, attention_part(): pl.pallas_call(attn_kernel, out_shape=(pltpu.VMEM((n_seqs, q_width), bf16...  13.4 us

profile of v4, /device:TPU:113, one launch (start us, length us, event | category | flops | bytes accessed | tf_op | source)
XLA Modules:
  0.0 91.5 jit_solution(7168204826148908423)
XLA Ops:
  0.6 13.4 %attn.1 = (bf16[128,512]{1,0:T(8,128)(2,1)S(1)}, bf16[128,128,128]{2,1,0:T(8,128)(2,1)}, bf16[128,128,128]{2,1,0:T(8,128)(2,1)}) custom-call(s32[128]{0:T(128)} %pos_s.1, bf16[128,5120]{1,0:T(8,128)(2,1)} %resid_ref.1, bf16[5120]{0:T(1024)(128)(2,1)} %gain_ref.2, s32[1,128]{1,0:T(1,128)} %bitcast.11, f32[1,128]{1,0:T(1,128)} %constant.2.clone.freq_ref, ...), custom_call_target="tpu_custom_call" | custom-call | flops 671088640 | bytes 30000000 | tf_op jit(solution)/shard_map/attn/pallas_call | solution.py:194
  14.1 76.4 %out_mlp.1 = bf16[128,5120]{1,0:T(8,128)(2,1)S(1)} custom-call(bf16[128,512]{1,0:T(8,128)(2,1)S(1)} %get-tuple-element.6.o_ref, bf16[128,5120]{1,0:T(8,128)(2,1)} %resid_ref.1, bf16[5120]{0:T(1024)(128)(2,1)} %gain_ref.3, bf16[512,5120]{1,0:T(8,128)(2,1)} %wo_ref.1, bf16[5120,4096]{1,0:T(8,128)(2,1)} %wg_ref.1, bf16[5120,4096]{1,0:T(8,128)(2,1)} %wu_ref.1, ...), custom_call_target="tpu_custom_call" | custom-call | flops 16106127360 | bytes 125829120 | tf_op jit(solution)/shard_map/out_mlp/pallas_call | solution.py:448
  90.5 1.1 %copy.20 = bf16[128,5120]{1,0:T(8,128)(2,1)} copy(bf16[128,5120]{1,0:T(8,128)(2,1)S(1)} %out_mlp.1) | data formatting | bytes 2621440

commit v5 on v4

--- a/solution.py
+++ b/solution.py
@@ -19,7 +19,7 @@
 BLK = 512
 SLOTS = 12
 SB = 8
-UNROLL = 4
+UNROLL = 8
 QCH = 5
 LAG_D, LAG_1, LAG_2 = 2, 7, 17
 GLAG_2, GLAG_3 = 3, 4
@@ -88,9 +88,6 @@
     for i in range(2, QCH):
         for c in w_copies(i):
             c.start()
-    for i in range(UNROLL):
-        k_in(i).start()
-        v_in(i).start()
     total = jnp.zeros((n_seqs, 1), f32)
     for i in range(QCH):
         x = resid_ref[:, i * kc:(i + 1) * kc].astype(f32)
@@ -100,7 +97,7 @@
         sl = slice(i * kc, (i + 1) * kc)
         normed[:, sl] = (resid_ref[:, sl].astype(f32) * inv * gain_ref[sl].astype(f32)[None]).astype(bf16)
 
-    for i in range(UNROLL, n_blk):
+    for i in range(n_blk):
         k_in(i).start()
         v_in(i).start()
 
@@ -287,6 +284,10 @@
         pltpu.make_async_copy(ring.at[slot], ring.at[slot], w_sem.at[slot]).wait()
         return slot
 
+    barrier = pltpu.get_barrier_semaphore()
+    for dev in (mate, first, second):
+        pl.semaphore_signal(barrier, inc=1, device_id={'tp': dev}, device_id_type=MESH)
+
     for b in range(n_fb):
         load_out(b, 0, b).start()
     for b in range(n_fb, n_ch):
@@ -299,9 +300,6 @@
         return c
     lax.fori_loop(2, SLOTS, first_loads, 0)
 
-    barrier = pltpu.get_barrier_semaphore()
-    for dev in (mate, first, second):
-        pl.semaphore_signal(barrier, inc=1, device_id={'tp': dev}, device_id_type=MESH)
     pl.semaphore_wait(barrier, 3)
 
     def at(t, lag, fn):

time: 91.7 us -> 92 us (level)
  no operation moved by 1% of the time
where the time goes in v5:
time: 92 us; the launch traced here: 91.8 us
  Pallas kernels  90.1 us (98%)
  local copies, waits for them, and re-layouts  1.06 us (1%)
    pallas_call x1, Pallas kernels, mlp_part(): pl.pallas_call(functools.partial(mlp_kernel, (n_ch, n_fb, rows)), out_sha...  76.1 us
    pallas_call x1, Pallas kernels, attention_part(): pl.pallas_call(attn_kernel, out_shape=(pltpu.VMEM((n_seqs, q_width), bf16...  14 us

profile of v5, /device:TPU:113, one launch (start us, length us, event | category | flops | bytes accessed | tf_op | source)
XLA Modules:
  0.0 91.8 jit_solution(7135494754359265291)
XLA Ops:
  0.6 14.0 %attn.1 = (bf16[128,512]{1,0:T(8,128)(2,1)S(1)}, bf16[128,128,128]{2,1,0:T(8,128)(2,1)}, bf16[128,128,128]{2,1,0:T(8,128)(2,1)}) custom-call(s32[128]{0:T(128)} %pos_s.1, bf16[128,5120]{1,0:T(8,128)(2,1)} %resid_ref.1, bf16[5120]{0:T(1024)(128)(2,1)} %gain_ref.2, s32[1,128]{1,0:T(1,128)} %bitcast.11, f32[1,128]{1,0:T(1,128)} %constant.2.clone.freq_ref, ...), custom_call_target="tpu_custom_call" | custom-call | flops 671088640 | bytes 30000000 | tf_op jit(solution)/shard_map/attn/pallas_call | solution.py:191
  14.6 76.1 %out_mlp.1 = bf16[128,5120]{1,0:T(8,128)(2,1)S(1)} custom-call(bf16[128,512]{1,0:T(8,128)(2,1)S(1)} %get-tuple-element.6.o_ref, bf16[128,5120]{1,0:T(8,128)(2,1)} %resid_ref.1, bf16[5120]{0:T(1024)(128)(2,1)} %gain_ref.3, bf16[512,5120]{1,0:T(8,128)(2,1)} %wo_ref.1, bf16[5120,4096]{1,0:T(8,128)(2,1)} %wg_ref.1, bf16[5120,4096]{1,0:T(8,128)(2,1)} %wu_ref.1, ...), custom_call_target="tpu_custom_call" | custom-call | flops 16106127360 | bytes 125829120 | tf_op jit(solution)/shard_map/out_mlp/pallas_call | solution.py:446
  90.8 1.1 %copy.20 = bf16[128,5120]{1,0:T(8,128)(2,1)} copy(bf16[128,5120]{1,0:T(8,128)(2,1)S(1)} %out_mlp.1) | data formatting | bytes 2621440
